TPU v7x, 32 devices: a whole 2x2x4 slice. The times are simulated.
32 devices in a mesh: tok: 16 (over z, y, x), head: 2 (over core).
Axes of the slice: x: 2, y: 2, z: 4, core: 2. Of those that a mesh axis runs over, the one named last changes fastest.
Arguments:
- text_queries: bfloat16 [256, 8192], P('tok', 'head'), may hold values from -6 to 6
- text_grads: bfloat16 [256, 8192], P('tok', 'head'), may hold values from -6 to 6
- vision_keys: bfloat16 [8192, 1024], P('tok', 'head'), may hold values from -6 to 6
- video_value_rows: bfloat16 [8192, 1024], P('tok', 'head'), may hold values from -6 to 6
- vision: bfloat16 [8192, 4096], P('tok'), may hold values from -6 to 6
- lengths: int32 [8], replicated, may hold values from 16 to 48, as said below
- frame_range: int32 [8, 2], replicated, may hold values from 0 to 64, as said below
Outputs:
- query_grad: bfloat16 [256, 8192], P(None, 'head')
- key_weight_grad: float32 [4096, 1024], P('tok', 'head')
- value_weight_grad: float32 [4096, 1024], P('tok', 'head')
Inputs may be any that keep to these rules, and one draw needn't show every extreme that they name: Each segment holds at least one row; the lengths sum to 256. `frame_range`: each segment's range covers 64 // 4 frames or more, first entry below the second.
All inputs are finite; a program needn't handle non-finite values.
Results may differ from a plain program's by a relative error of at most 0.0073.
Values may be sent and summed in bfloat16 or wider, within the bound.
A program may use at most 128 MiB of HBM per device.

v0:
```python
import jax
import jax.numpy as jnp
from jax import lax
from jax.sharding import PartitionSpec as P

HEAD_WIDTH = 128
FRAME_DEV = 4
NEG_FILL = -1e30


def shards(text_queries, text_grads, vision_keys, video_value_rows, vision, lengths, frame_range):
    feature_block = lax.all_to_all(vision, "tok", split_axis=1, concat_axis=0, tiled=True)
    text_q, text_g = (
        lax.all_gather(text_queries, "tok", axis=0, tiled=True),
        lax.all_gather(text_grads, "tok", axis=0, tiled=True),
    )
    text_len = text_q.shape[0]
    kv_rows = vision_keys.shape[0]
    kv_local = vision_keys.shape[1] // HEAD_WIDTH
    group_width = text_q.shape[1] // vision_keys.shape[1]
    score_scale = HEAD_WIDTH ** (-0.5)
    row_ids = jnp.arange(text_len, dtype=jnp.int32)
    segment_ends = jnp.cumsum(lengths)
    segment = jnp.sum((row_ids[:, None] >= segment_ends[None, :]).astype(jnp.int32), axis=1)
    segment_pick = (
        segment[:, None] == jnp.arange(lengths.shape[0], dtype=jnp.int32)[None, :]
    ).astype(jnp.int32)
    first_frame = jnp.sum(segment_pick * frame_range[None, :, 0], axis=1)
    end_frame = jnp.sum(segment_pick * frame_range[None, :, 1], axis=1)
    key_ids = lax.axis_index("tok") * kv_rows + jnp.arange(kv_rows, dtype=jnp.int32)
    frames = key_ids // (kv_rows // FRAME_DEV)
    allowed = (frames[None, :] >= first_frame[:, None]) & (frames[None, :] < end_frame[:, None])
    query_member = text_q.reshape(text_len, kv_local, group_width, HEAD_WIDTH).transpose(2, 0, 1, 3)
    grad_member = text_g.reshape(text_len, kv_local, group_width, HEAD_WIDTH).transpose(2, 0, 1, 3)
    key_three = vision_keys.reshape(kv_rows, kv_local, HEAD_WIDTH)
    value_three = video_value_rows.reshape(kv_rows, kv_local, HEAD_WIDTH)

    def scores_of(query_one, grad_one):
        scores = (
            jnp.einsum("ihd,jhd->hij", query_one, key_three, preferred_element_type=jnp.float32)
            * score_scale
        )
        dprobs = jnp.einsum(
            "ihd,jhd->hij", grad_one, value_three, preferred_element_type=jnp.float32
        )
        return (scores, dprobs)

    def local_stats(carry, member):
        scores, dprobs = scores_of(member[0], member[1])
        local_max = jnp.max(jnp.where(allowed, scores, NEG_FILL), axis=2)
        local_exp = jnp.where(allowed, jnp.exp(scores - local_max[..., None]), 0.0)
        return (carry, (local_max, jnp.sum(local_exp, axis=2), jnp.sum(local_exp * dprobs, axis=2)))

    unused, (local_max, local_sum, local_dot) = lax.scan(
        local_stats, jnp.zeros((), jnp.float32), (query_member, grad_member)
    )
    row_max = lax.pmax(local_max, "tok")
    rescale = jnp.exp(local_max - row_max)
    row_sum, row_dot = lax.psum((local_sum * rescale, local_dot * rescale), "tok")

    def member_grads(running, member):
        query_one, grad_one, max_one, sum_one, dot_one = member
        scores, dprobs = scores_of(query_one, grad_one)
        exp_terms = jnp.where(allowed, jnp.exp(scores - max_one[..., None]), 0.0)
        attn_probs = exp_terms / sum_one[..., None]
        row_delta = dot_one / sum_one
        dscore = (attn_probs * (dprobs - row_delta[..., None])).astype(jnp.bfloat16)
        value_sum = running[1] + jnp.einsum(
            "hij,ihd->jhd",
            attn_probs.astype(jnp.bfloat16),
            grad_one,
            preferred_element_type=jnp.float32,
        )
        key_sum = running[0] + jnp.einsum(
            "hij,ihd->jhd", dscore, query_one, preferred_element_type=jnp.float32
        )
        query_part = score_scale * jnp.einsum(
            "hij,jhd->ihd", dscore, key_three, preferred_element_type=jnp.float32
        )
        return ((key_sum, value_sum), query_part)

    zero_acc = jnp.zeros((kv_rows, kv_local, HEAD_WIDTH), jnp.float32)
    (key_sum, value_sum), query_parts = lax.scan(
        member_grads, (zero_acc, zero_acc), (query_member, grad_member, row_max, row_sum, row_dot)
    )
    key_grad = (score_scale * key_sum).astype(jnp.bfloat16)
    value_grad = value_sum.astype(jnp.bfloat16)
    query_part = query_parts.transpose(1, 2, 0, 3).reshape(text_len, -1)
    query_grad = lax.psum(query_part, "tok").astype(jnp.bfloat16)
    kv_data = jnp.concatenate(
        (key_grad.reshape(kv_rows, -1), value_grad.reshape(kv_rows, -1)), axis=1
    )
    half_width = kv_data.shape[1] // 2
    weight_grads = jnp.einsum(
        "tf,tc->fc",
        feature_block,
        lax.all_gather(kv_data, "tok", axis=0, tiled=True),
        preferred_element_type=jnp.float32,
    )
    return (query_grad, weight_grads[:, :half_width], weight_grads[:, half_width:])


def solution(mesh):
    return jax.shard_map(
        shards,
        mesh=mesh,
        in_specs=(
            P("tok", "head"),
            P("tok", "head"),
            P("tok", "head"),
            P("tok", "head"),
            P("tok", None),
            P(),
            P(),
        ),
        out_specs=(P(None, "head"), P("tok", "head"), P("tok", "head")),
        check_vma=False,
    )
```

profile of v0, /device:TPU:4, one launch (start us, length us, event | category | flops | bytes accessed | tf_op | source)
XLA Modules:
  0.0 843.1 jit_solution(17630682502274391698)
XLA Ops:
  11.8 60.5 %all-gather.4.cloned.1.call-done = bf16[256,4096]{1,0:T(8,128)(2,1)} async-done(((bf16[16,4096]{1,0:T(8,128)(2,1)}), bf16[256,4096]{1,0:T(8,128)(2,1)}) %all-gather.4.cloned.1.call-update) | async-done | bytes 2097168 | tf_op jit(solution)/shard_map/all_gather | solution.py:14
  72.4 4.1 copy.72
  76.4 3.0 copy.80
  79.5 54.9 %all-gather.6.cloned.1.call-done = bf16[256,4096]{1,0:T(8,128)(2,1)} async-done(((bf16[16,4096]{1,0:T(8,128)(2,1)}), bf16[256,4096]{1,0:T(8,128)(2,1)}) %all-gather.6.cloned.1.call-update) | async-done | bytes 2097168 | tf_op jit(solution)/shard_map/all_gather | solution.py:15
  134.3 4.1 copy.74
  138.4 4.0 copy.78
  142.4 26.8 %while.30 = (s32[]{:T(128)}, f32[8,4,256]{2,1,0:T(4,128)S(1)}, f32[8,4,256]{2,1,0:T(4,128)S(1)}, f32[8,4,256]{2,1,0:T(4,128)S(1)}, bf16[8,256,4,128]{3,1,2,0:T(8...) while((s32[]{:T(128)}, f32[8,4,256]{2,1,0:T(4,128)S(1)}, ...), condition=%wide.region_8.9_spmd.clone, body=%wide.region_4.8_spmd.clone.sunk | while | flops 275117056 | bytes 8437901 | solution.py:54
  143.9 1.8 multiply_reduce_fusion.2
  147.2 1.8 multiply_reduce_fusion.2
  150.6 1.8 multiply_reduce_fusion.2
  153.9 1.8 multiply_reduce_fusion.2
  157.3 1.8 multiply_reduce_fusion.2
  160.6 1.8 multiply_reduce_fusion.2
  164.0 1.8 multiply_reduce_fusion.2
  167.4 1.8 multiply_reduce_fusion.2
  169.2 71.0 %pmax.7 = f32[8,4,256]{2,1,0:T(4,128)S(1)} all-reduce(f32[8,4,256]{2,1,0:T(4,128)S(1)} %get-tuple-element.116), channel_id=1, replica_groups=mesh['tok'=16,'head'=2] {'tok'}, use_global_device_ids=true, to_apply=%region_9.10 | all-reduce | flops 8192 | bytes 65536 | tf_op jit(solution)/shard_map/pmax | solution.py:57
  241.0 103.4 %all-reduce.4.cloned.1.call-done = (f32[8,4,256]{2,1,0:T(4,128)}, f32[8,4,256]{2,1,0:T(4,128)}) async-done(((f32[8,4,256]{2,1,0:T(4,128)}, f32[8,4,256]{2,1,0:T(4,128)}), (f32[8,4,256]{2,1,0:T(4,128)}, f32[8,4,256]{2,1,0:T(4,128)})) %all-reduce.4.cloned.1.call-update) | async-done | bytes 65552 | tf_op jit(solution)/shard_map/psum | solution.py:59
  344.4 69.9 %while.31 = (s32[]{:T(128)}, f32[512,4,128]{0,2,1:T(8,128)S(1)}, f32[512,4,128]{0,2,1:T(8,128)S(1)}, f32[8,256,4,128]{3,1,2,0:T(8,128)}, bf16[8,256,4,128]{3,1,2...) while((s32[]{:T(128)}, f32[512,4,128]{0,2,1:T(8,128)S(1)}, ...), condition=%wide.region_13.14_spmd.clone, body=%wide.region_12.13_spmd.clone.sunk | while | flops 676856832 | bytes 17084612 | solution.py:83
  346.0 1.7 select_divide_fusion.2
  347.7 1.4 multiply_convert_fusion.3
  349.1 1.4 fusion.76
  354.8 1.7 select_divide_fusion.2
  356.5 1.4 multiply_convert_fusion.3
  357.9 1.4 fusion.76
  363.5 1.7 select_divide_fusion.2
  365.2 1.4 multiply_convert_fusion.3
  366.7 1.4 fusion.76
  372.3 1.7 select_divide_fusion.2
  374.0 1.4 multiply_convert_fusion.3
  375.4 1.4 fusion.76
  381.0 1.7 select_divide_fusion.2
  384.1 1.4 fusion.76
  389.7 1.7 select_divide_fusion.2
  391.4 1.4 multiply_convert_fusion.3
  392.8 1.4 fusion.76
  398.4 1.7 select_divide_fusion.2
  400.1 1.4 multiply_convert_fusion.3
  401.6 1.4 fusion.76
  407.1 1.7 select_divide_fusion.2
  410.2 1.4 fusion.76
  415.6 6.5 copy.85
  422.1 5.2 all-to-all-start
  427.3 4.6 copy.84
  431.9 5.8 copy.93
  437.7 350.3 %all-reduce.5 = bf16[256,4096]{1,0:T(8,128)(2,1)} all-reduce(f32[256,4096]{1,0:T(8,128)} %bitcast.132), channel_id=1, replica_groups=mesh['tok'=16,'head'=2] {'tok'}, use_global_device_ids=true, to_apply=%region_14.15 | all-reduce | flops 1048576 | bytes 6291456 | tf_op jit(solution)/shard_map/psum | solution.py:89
  788.0 6.4 copy.86
  794.4 30.8 %all-gather.8.cloned.1.call-done = bf16[8192,1024]{0,1:T(8,128)(2,1)} async-done(((bf16[512,1024]{0,1:T(8,128)(2,1)}), bf16[8192,1024]{0,1:T(8,128)(2,1)}) %all-gather.8.cloned.1.call-update) | async-done | bytes 16777232 | tf_op jit(solution)/shard_map/all_gather | solution.py:97
  825.2 9.3 %convolution_bitcast_fusion.2 = f32[256,1024]{0,1:T(8,128)S(1)} fusion(bf16[8192,1024]{0,1:T(8,128)(2,1)} %all-gather.8.cloned.1.call-done, bf16[8192,256]{1,0:T(8,128)(2,1)} %bitcast.136), kind=kOutput, calls=%fused_computation.44 | convolution fusion | flops 4294967296 | bytes 22020096 | tf_op jit(solution)/shard_map/tf,tc->fc/dot_general | solution.py:94
  (119 shorter events, 57.2 us)
Async XLA Ops:
  7.2 4.0 copy-start.1
  7.2 65.2 %all-gather.4.cloned.1.call-start = ((), (), s32[]{:S(2)}) async-start(), calls=%async_computation.1 | async-start | bytes 2228224 | tf_op jit(solution)/shard_map/all_gather | solution.py:14
  7.9 126.4 %all-gather.6.cloned.1.call-start = ((), (), s32[]{:S(2)}) async-start(), calls=%async_computation.2 | async-start | bytes 2228224 | tf_op jit(solution)/shard_map/all_gather | solution.py:15
  8.7 335.8 %all-reduce.4.cloned.1.call-start = ((), (), s32[]{:S(2)}) async-start(), calls=%async_computation.4 | async-start | bytes 131072 | tf_op jit(solution)/shard_map/psum | solution.py:59
  9.6 2.2 copy-start.2
  169.2 71.8 %copy-start = (bf16[8,256,4,128]{3,1,2,0:T(8,128)(2,1)}, bf16[8,256,4,128]{3,1,2,0:T(8,128)(2,1)S(1)}, u32[]{:S(2)}) copy-start(bf16[8,256,4,128]{3,1,2,0:T(8,128)(2,1)S(1)} %get-tuple-element.641) | copy-start | bytes 6291460
  240.9 584.3 %all-gather.8.cloned.1.call-start = ((), (), s32[]{:S(2)}) async-start(), calls=%async_computation.3 | async-start | bytes 17825792 | tf_op jit(solution)/shard_map/all_gather | solution.py:97
  422.1 365.9 %all-to-all-start = ((bf16[512,16,256]{0,2,1:T(8,128)(2,1)}), bf16[512,16,256]{0,2,1:T(8,128)(2,1)}, u32[]{:S(2)}, u32[]{:S(2)}) async-start(bf16[512,16,256]{0,2,1:T(8,128)(2,1)} %bitcast.130), calls=%async_computation | async-start | bytes 8388608 | tf_op jit(solution)/shard_map/all_to_all | solution.py:12
Sparse Core Ops, SparseCore 0:
  10.8 61.5 all-gather.3
  75.1 59.1 all-gather.5
  241.0 103.3 all-reduce.3
  415.8 409.3 all-gather.7
where the time goes:
time: 846 us; the launch traced here: 843 us
  blocking collectives  421 us (50%)
  waiting for transfers between devices  251 us (30%)
  matrix products  85.4 us (10%)
  local copies, waits for them, and re-layouts  48.1 us (6%)
  other arithmetic  17.4 us (2%)
  between operations  13.9 us (2%)
    psum x1, blocking collectives, shards(): query_grad = lax.psum(query_part, 'tok').astype(jnp.bfloat16)  350 us
    psum x1, waiting for transfers between devices, shards(): lax.psum((local_sum * rescale, local_dot * rescale), 'tok')  103 us
    pmax x1, blocking collectives, shards(): row_max = lax.pmax(local_max, 'tok')  71 us
    all_gather x1, waiting for transfers between devices, shards(): lax.all_gather(text_queries, 'tok', axis=0, tiled=True)  60.5 us
    all_gather x1, waiting for transfers between devices, shards(): lax.all_gather(text_grads, 'tok', axis=0, tiled=True)  54.9 us
    all_gather x1, waiting for transfers between devices, shards(): lax.all_gather(kv_data, 'tok', axis=0, tiled=True)  30.8 us
    dot_general x16, matrix products, scores_of(): jnp.einsum('ihd,jhd->hij', grad_one, value_three, preferred_element_type=...  25.6 us
    unnamed x16, local copies, waits for them, and re-layouts  23.2 us
  transfers between devices with their start and end apart: 5, of which 4 were waited for; matrix products, arithmetic and copies ran while one was open for 4% of the time, Pallas kernels for 0%

commit v1 on v0

--- a/solution.py
+++ b/solution.py
@@ -86,7 +86,7 @@
     key_grad = (score_scale * key_sum).astype(jnp.bfloat16)
     value_grad = value_sum.astype(jnp.bfloat16)
     query_part = query_parts.transpose(1, 2, 0, 3).reshape(text_len, -1)
-    query_grad = lax.psum(query_part, "tok").astype(jnp.bfloat16)
+    query_grad = jnp.sum(lax.all_gather(query_part, "tok"), axis=0).astype(jnp.bfloat16)
     kv_data = jnp.concatenate(
         (key_grad.reshape(kv_rows, -1), value_grad.reshape(kv_rows, -1)), axis=1
     )

time: 846 us -> 1470 us (1.74)
  waiting for transfers between devices: 251 us -> 976 us
  blocking collectives: 421 us -> 229 us
  matrix products: 85.4 us -> 124 us
  local copies, waits for them, and re-layouts: 48.1 us -> 78.9 us
  other arithmetic: 17.4 us -> 40.8 us
    all_gather x0 -> x1, waiting for transfers between devices: none -> 658 us  [shards(): lax.all_gather(query_part, 'tok')]
    psum x1 -> x0, blocking collectives: 350 us -> none  [shards(): query_grad = lax.psum(query_part, 'tok').astype(jnp.bfloat16)]
    all_to_all x0 -> x1, blocking collectives: none -> 158 us  [shards(): lax.all_to_all(vision, 'tok', split_axis=1, concat_axis=0, tiled=True)]
    all_gather x1, waiting for transfers between devices: 30.8 us -> 96.8 us  [shards(): lax.all_gather(kv_data, 'tok', axis=0, tiled=True)]
    dynamic_update_slice x0 -> x16, local copies, waits for them, and re-layouts: none -> 31.8 us  [shards(): lax.scan(member_grads, (zero_acc, zero_acc), (query_member, grad_member,...]
    reduce_sum x0 -> x1, other arithmetic: none -> 21.1 us  [shards(): jnp.sum(lax.all_gather(query_part, 'tok'), axis=0).astype(jnp.bfloat16)]
  transfers between devices with their start and end apart: 5 -> 5, of which waited for: 4 -> 5; matrix products, arithmetic and copies ran while one was open for 4% -> 3% of each run, Pallas kernels for 0% -> 0%
where the time goes in v1:
time: 1470 us; the launch traced here: 1460 us
  waiting for transfers between devices  976 us (66%)
  blocking collectives  229 us (16%)
  matrix products  124 us (8%)
  local copies, waits for them, and re-layouts  78.9 us (5%)
  other arithmetic  40.8 us (3%)
    all_gather x1, waiting for transfers between devices, shards(): lax.all_gather(query_part, 'tok')  658 us
    all_to_all x1, blocking collectives, shards(): lax.all_to_all(vision, 'tok', split_axis=1, concat_axis=0, tiled=True)  158 us
    psum x1, waiting for transfers between devices, shards(): lax.psum((local_sum * rescale, local_dot * rescale), 'tok')  103 us
    all_gather x1, waiting for transfers between devices, shards(): lax.all_gather(kv_data, 'tok', axis=0, tiled=True)  96.8 us
    pmax x1, blocking collectives, shards(): row_max = lax.pmax(local_max, 'tok')  71 us
    all_gather x1, waiting for transfers between devices, shards(): lax.all_gather(text_grads, 'tok', axis=0, tiled=True)  59.8 us
    all_gather x1, waiting for transfers between devices, shards(): lax.all_gather(text_queries, 'tok', axis=0, tiled=True)  56.3 us
    dynamic_update_slice x16, local copies, waits for them, and re-layouts, shards(): lax.scan(member_grads, (zero_acc, zero_acc), (query_member, grad_member,...  31.8 us
  transfers between devices with their start and end apart: 5, of which 5 were waited for; matrix products, arithmetic and copies ran while one was open for 3% of the time, Pallas kernels for 0%

profile of v1, /device:TPU:4, one launch (start us, length us, event | category | flops | bytes accessed | tf_op | source)
XLA Modules:
  0.0 1463.8 jit_solution(2744324950203863461)
XLA Ops:
  12.5 59.8 %all-gather.7.cloned.1.call-done = bf16[256,4096]{1,0:T(8,128)(2,1)} async-done(((bf16[16,4096]{1,0:T(8,128)(2,1)}), bf16[256,4096]{1,0:T(8,128)(2,1)}) %all-gather.7.cloned.1.call-update) | async-done | bytes 2097168 | tf_op jit(solution)/shard_map/all_gather | solution.py:15
  72.4 3.3 copy.76
  75.6 2.4 copy.80
  78.0 56.3 %all-gather.5.cloned.1.call-done = bf16[256,4096]{1,0:T(8,128)(2,1)} async-done(((bf16[16,4096]{1,0:T(8,128)(2,1)}), bf16[256,4096]{1,0:T(8,128)(2,1)}) %all-gather.5.cloned.1.call-update) | async-done | bytes 2097168 | tf_op jit(solution)/shard_map/all_gather | solution.py:14
  134.3 3.3 copy.74
  137.6 2.4 copy.82
  140.0 35.8 %while.30 = (s32[]{:T(128)}, f32[8,4,256]{2,1,0:T(4,128)S(1)}, f32[8,4,256]{2,1,0:T(4,128)S(1)}, f32[8,4,256]{2,1,0:T(4,128)S(1)}, bf16[8,256,4,128]{3,1,2,0:T(8...) while((s32[]{:T(128)}, f32[8,4,256]{2,1,0:T(4,128)S(1)}, ...), condition=%wide.region_8.9_spmd.clone, body=%wide.region_4.8_spmd.clone.sunk | while | flops 275117056 | bytes 8438909 | solution.py:54
  175.8 71.0 %pmax.7 = f32[8,4,256]{2,1,0:T(4,128)S(1)} all-reduce(f32[8,4,256]{2,1,0:T(4,128)S(1)} %get-tuple-element.116), channel_id=1, replica_groups=mesh['tok'=16,'head'=2] {'tok'}, use_global_device_ids=true, to_apply=%region_9.10 | all-reduce | flops 8192 | bytes 65536 | tf_op jit(solution)/shard_map/pmax | solution.py:57
  247.6 103.5 %all-reduce.3.cloned.1.call-done = (f32[8,4,256]{2,1,0:T(4,128)}, f32[8,4,256]{2,1,0:T(4,128)}) async-done(((f32[8,4,256]{2,1,0:T(4,128)}, f32[8,4,256]{2,1,0:T(4,128)}), (f32[8,4,256]{2,1,0:T(4,128)}, f32[8,4,256]{2,1,0:T(4,128)})) %all-reduce.3.cloned.1.call-update) | async-done | bytes 65552 | tf_op jit(solution)/shard_map/psum | solution.py:59
  351.1 131.5 %while.31 = (s32[]{:T(128)}, f32[512,4,128]{0,2,1:T(8,128)}, f32[512,4,128]{0,2,1:T(8,128)}, f32[8,256,4,128]{1,3,0,2:T(8,128)}, bf16[8,256,4,128]{3,1,2,0:T(8,1...) while((s32[]{:T(128)}, f32[512,4,128]{0,2,1:T(8,128)}, ...), condition=%wide.region_13.14_spmd.clone, body=%wide.region_12.13_spmd.clone.sunk | while | flops 676856832 | bytes 23378656 | solution.py:83
  355.9 2.3 fusion.76
  358.2 2.1 copy.101
  362.2 2.3 fusion.74
  364.5 2.3 fusion.75
  371.7 2.3 fusion.76
  374.0 2.1 copy.101
  378.0 2.7 fusion.74
  380.7 2.7 fusion.75
  388.2 2.3 fusion.76
  390.5 2.1 copy.101
  394.5 2.7 fusion.74
  397.2 2.7 fusion.75
  404.7 2.3 fusion.76
  407.1 2.1 copy.101
  411.1 2.7 fusion.74
  413.7 2.7 fusion.75
  421.3 2.3 fusion.76
  427.6 2.7 fusion.74
  430.2 2.7 fusion.75
  437.8 2.3 fusion.76
  444.1 2.7 fusion.74
  446.8 2.7 fusion.75
  454.3 2.3 fusion.76
  460.6 2.7 fusion.74
  463.3 2.7 fusion.75
  470.8 2.3 fusion.76
  477.1 2.7 fusion.74
  479.8 2.7 fusion.75
  486.3 5.6 copy.87
  491.9 6.6 copy.89
  498.6 158.1 %all_to_all.19 = bf16[512,16,256]{0,2,1:T(8,128)(2,1)} all-to-all(bf16[512,16,256]{0,2,1:T(8,128)(2,1)} %bitcast.126), channel_id=1, replica_groups=mesh['tok'=16,'head'=2] {'tok'}, dimensions={1} | all-to-all | bytes 8388608 | tf_op jit(solution)/shard_map/all_to_all | solution.py:12
  656.7 6.5 copy.90
  663.2 96.8 %all-gather.11.cloned.1.call-done = bf16[8192,1024]{0,1:T(8,128)(2,1)} async-done(((bf16[512,1024]{0,1:T(8,128)(2,1)}), bf16[8192,1024]{0,1:T(8,128)(2,1)}) %all-gather.11.cloned.1.call-update) | async-done | bytes 16777232 | tf_op jit(solution)/shard_map/all_gather | solution.py:97
  760.0 9.3 convolution_bitcast_fusion.2
  771.4 658.2 %all-gather.9.cloned.1.call-done = f32[16,256,4096]{2,1,0:T(8,128)} async-done(((f32[1,256,4096]{2,1,0:T(8,128)}), f32[16,256,4096]{2,1,0:T(8,128)}) %all-gather.9.cloned.1.call-update) | async-done | bytes 67108880 | tf_op jit(solution)/shard_map/all_gather | solution.py:89
  1429.6 21.1 %reduce_sum.57 = bf16[256,4096]{1,0:T(8,128)(2,1)S(1)} reduce(f32[16,256,4096]{2,1,0:T(8,128)} %all-gather.9.cloned.1.call-done, f32[]{:T(128)} %constant.66.clone.1), dimensions={0}, to_apply=%region_14.15 | reduce | flops 15728640 | bytes 69206016 | tf_op jit(solution)/shard_map/reduce_sum | solution.py:89
  1450.7 2.5 copy.98
  1453.2 4.1 copy.91
  (168 shorter events, 109.3 us)
Async XLA Ops:
  7.2 4.7 copy-start.2
  7.2 65.2 %all-gather.7.cloned.1.call-start = ((), (), s32[]{:S(2)}) async-start(), calls=%async_computation.2 | async-start | bytes 2228224 | tf_op jit(solution)/shard_map/all_gather | solution.py:15
  7.9 126.4 %all-gather.5.cloned.1.call-start = ((), (), s32[]{:S(2)}) async-start(), calls=%async_computation.1 | async-start | bytes 2228224 | tf_op jit(solution)/shard_map/all_gather | solution.py:14
  8.7 342.4 %all-reduce.3.cloned.1.call-start = ((), (), s32[]{:S(2)}) async-start(), calls=%async_computation.5 | async-start | bytes 131072 | tf_op jit(solution)/shard_map/psum | solution.py:59
  9.6 2.9 copy-start.3
  247.5 512.5 %all-gather.11.cloned.1.call-start = ((), (), s32[]{:S(2)}) async-start(), calls=%async_computation.4 | async-start | bytes 17825792 | tf_op jit(solution)/shard_map/all_gather | solution.py:97
  351.1 2.6 copy-start
  364.5 2.4 copy-start.1
  366.8 2.6 copy-start
  380.7 2.7 copy-start.1
  383.4 2.6 copy-start
  397.2 2.7 copy-start.1
  399.9 2.6 copy-start
  413.7 2.7 copy-start.1
  416.4 2.6 copy-start
  430.2 2.7 copy-start.1
  432.9 2.6 copy-start
  446.8 2.7 copy-start.1
  449.5 2.6 copy-start
  463.3 2.7 copy-start.1
  466.0 2.6 copy-start
  479.8 2.7 copy-start.1
  486.2 943.4 %all-gather.9.cloned.1.call-start = ((), (), s32[]{:S(2)}) async-start(), calls=%async_computation.3 | async-start | bytes 71303168 | tf_op jit(solution)/shard_map/all_gather | solution.py:89
Sparse Core Ops, SparseCore 0:
  10.8 61.5 all-gather.6
  75.1 59.1 all-gather.4
  247.6 103.3 all-reduce.2
  486.3 273.6 all-gather.10
  762.6 666.8 all-gather.8
